TPU v7x, 32 devices: a whole 2x2x4 slice. The times are simulated.
32 devices in a mesh: stream: 8 (over y, x, core), cross: 4 (over z).
Axes of the slice: x: 2, y: 2, z: 4, core: 2. Of those that a mesh axis runs over, the one named last changes fastest.
Arguments:
- latents: bfloat16 [16384, 128], P(('stream', 'cross')), may hold values from -6 to 6
- stale_latents: bfloat16 [16384, 128], P(('stream', 'cross')), may hold values from -6 to 6
- edge_latents: bfloat16 [49152, 128], P(('stream', 'cross')), may hold values from -6 to 6
- senders: int32 [49152], P(('stream', 'cross')), may hold values from 0 to 1023
- receivers: int32 [49152], P(('stream', 'cross')), may hold values from 0 to 511
- edge_count: int32 [32], P(('stream', 'cross')), may hold values from 512 to 1536, as said below
- send_list: int32 [32, 4, 128], P(('stream', 'cross')), may hold values from 0 to 511
- node_cotangent: bfloat16 [16384, 128], P(('stream', 'cross')), may hold values from -6 to 6
- edge_cotangent: bfloat16 [49152, 128], P(('stream', 'cross')), may hold values from -6 to 6
- edge_first: bfloat16 [384, 128], replicated, may hold values from -0.3125 to 0.3125
- edge_bias: float32 [128], replicated, may hold values from -3 to 3
- edge_second: bfloat16 [128, 128], replicated, may hold values from -0.5 to 0.5
- edge_gain: float32 [128], replicated, may hold values from 0.25 to 1.75
- node_first: bfloat16 [256, 128], replicated, may hold values from -0.375 to 0.375
- node_bias: float32 [128], replicated, may hold values from -3 to 3
- node_second: bfloat16 [128, 128], replicated, may hold values from -0.5 to 0.5
- node_gain: float32 [128], replicated, may hold values from 0.25 to 1.75
Outputs:
- new_latents: bfloat16 [16384, 128], P(('stream', 'cross'))
- latent_grads: bfloat16 [16384, 128], P(('stream', 'cross'))
- stale_grads: bfloat16 [16384, 128], P(('stream', 'cross'))
- edge_grads: bfloat16 [49152, 128], P(('stream', 'cross'))
- edge_first_grad: float32 [384, 128], replicated
- edge_bias_grad: float32 [128], replicated
- edge_second_grad: float32 [128, 128], replicated
- edge_gain_grad: float32 [128], replicated
- node_first_grad: float32 [256, 128], replicated
- node_bias_grad: float32 [128], replicated
- node_second_grad: float32 [128, 128], replicated
- node_gain_grad: float32 [128], replicated
Inputs may be any that keep to these rules, and one draw needn't show every extreme that they name: `edge_count`: a partition's live edge slots come first; some partition has 1536 live slots. `senders`: rows below 512 are the partition's own nodes, the rest its four halo blocks in the order of the steps. `send_list`: a row may be listed more than once.
All inputs are finite; a program needn't handle non-finite values.
Results may differ from a plain program's by a relative error of at most 0.015.
Values may be sent and summed in bfloat16 or wider, within the bound.
No kernel may reach another device: no remote copies, remote signals or barrier semaphores. Data moves between devices by JAX's collectives and lax.ppermute only.
A program may use at most 64 MiB of HBM per device.

v0:
```python
import functools
import math

import jax
import jax.numpy as jnp
from jax import lax
from jax.experimental import pallas as pl
from jax.experimental.pallas import tpu as pltpu
from jax.sharding import PartitionSpec as P


EPSILON = 1e-05
BF = jnp.bfloat16
F32 = jnp.float32
VMEM_LIMIT = 40 * 1024 * 1024


def mm(a, b):
    return jnp.dot(a, b, preferred_element_type=F32)


def mm_nt(a, b):
    return lax.dot_general(a, b, (((1,), (1,)), ((), ())), preferred_element_type=F32)


def mm_tn(a, b):
    return lax.dot_general(a, b, (((0,), (0,)), ((), ())), preferred_element_type=F32)


def index_columns(index_ref, row):
    line = index_ref[pl.ds(row, 1), :].astype(F32)
    return jnp.broadcast_to(line, (line.shape[1], line.shape[1])).T


I16 = jnp.int16


def ones_where(mask, shape):
    return jnp.where(mask, jnp.ones(shape, BF), jnp.zeros(shape, BF))


def one_hot_rows(column, size):
    lanes = column.shape[1]
    lane = lax.broadcasted_iota(jnp.int32, column.shape, 1)
    short = column.astype(jnp.int32).astype(I16)
    blocks = [
        ones_where(short == (lane + base).astype(I16), column.shape)
        for base in range(0, size, lanes)
    ]
    return jnp.concatenate(blocks, axis=1)


def one_hot_columns(index_ref, row, size, fold=False):
    line = index_ref[pl.ds(row, 1), :]
    if fold:
        line = jnp.where(line >= size, line - size, line)
    shape = (size, line.shape[1])
    tile = jnp.broadcast_to(line, (16, line.shape[1])).astype(I16)
    place = lax.broadcasted_iota(jnp.int32, shape, 0).astype(I16)
    return ones_where(place == jnp.concatenate([tile] * (size // 16), axis=0), shape)


def folded(column, half):
    upper = column >= float(half)
    return jnp.where(upper, column - float(half), column), upper


def side_by_side(rows):
    half = rows.shape[0] // 2
    return jnp.concatenate([rows[:half], rows[half:]], axis=1)


def stacked(pair):
    width = pair.shape[1] // 2
    return jnp.concatenate([pair[:, :width], pair[:, width:]], axis=0)


def chosen(pair, upper):
    width = pair.shape[1] // 2
    return jnp.where(upper, pair[:, width:], pair[:, :width])


def parted(rows, upper):
    zero = jnp.zeros_like(rows)
    return jnp.concatenate([jnp.where(upper, zero, rows), jnp.where(upper, rows, zero)], axis=1)


def parities():
    return (lax.rem(lax.axis_index("stream"), 2), lax.rem(lax.axis_index("cross"), 2))


def inner(axis):
    place = lax.axis_index(axis)
    return jnp.logical_and(place > 0, place < lax.axis_size(axis) - 1)


def list_order():
    odd_s, odd_c = parities()
    return (odd_s, 1 - odd_s, 2 + odd_c, 3 - odd_c)


def load_kernel(list_hbm, stale_hbm, *rest):
    count = (len(rest) - 5 - 2) // 2
    sources = rest[:count]
    outs = rest[count : count + 4]
    lists = rest[count + 4]
    kept = rest[count + 5 : 2 * count + 5]
    stale, sems = rest[2 * count + 5 :]
    copies = [
        pltpu.make_async_copy(a, b, sems.at[i])
        for i, (a, b) in enumerate(
            zip((list_hbm, stale_hbm) + sources, (lists, stale) + kept)
        )
    ]
    for copy in copies:
        copy.start()
    copies[0].wait()
    columns = [index_columns(lists, row) for row in list_order()]
    copies[1].wait()
    for column, out in zip(columns, outs):
        out[...] = mm(one_hot_rows(column, stale.shape[0]), stale[...]).astype(BF)
    for copy in copies[2:]:
        copy.wait()


def stale_kernel(list_ref, b0, b1, b2, b3, out_ref):
    total = None
    keep = (None, inner("stream"), None, inner("cross"))
    for row, part, valid in zip(list_order(), (b0, b1, b2, b3), keep):
        hot = one_hot_columns(list_ref, row, out_ref.shape[0])
        part = part[...]
        if valid is not None:
            part = jnp.where(valid, part, jnp.zeros_like(part))
        piece = mm(hot, part)
        total = piece if total is None else total + piece
    out_ref[...] = total.astype(BF)


def norm_forward(z):
    mean = jnp.mean(z, axis=-1, keepdims=True)
    centered = z - mean
    variance = jnp.mean(centered * centered, axis=-1, keepdims=True)
    inverse = lax.rsqrt(variance + EPSILON)
    return centered * inverse, jnp.broadcast_to(inverse, z.shape)


def norm_backward(slope, unit, inverse):
    first = jnp.mean(slope, axis=-1, keepdims=True)
    second = jnp.mean(slope * unit, axis=-1, keepdims=True)
    return inverse * (slope - first - unit * second)


def silu_pair(v):
    sig = 0.5 * jnp.tanh(0.5 * v) + 0.5
    hidden = v * sig
    return hidden, sig + hidden * (1.0 - sig)


def main_kernel(
    count_ref,
    latents,
    h0,
    h1,
    h2,
    h3,
    edges,
    senders,
    receivers,
    node_cot,
    edge_cot,
    edge_first,
    edge_bias,
    edge_second,
    edge_gain,
    node_first,
    node_bias,
    node_second,
    node_gain,
    new_latents,
    latent_grads,
    edge_grads,
    g0,
    g1,
    g2,
    g3,
    packed,
    table,
    hot_recv,
    turn_recv,
    turn_send,
    joined,
    hidden_s,
    slope_s,
    unit_s,
    inverse_s,
    upper_send,
    upper_recv,
    alive_edges,
    dz_s,
    dpre_s,
    dpre_send,
    dpre_recv,
    latent_out,
    grad_out,
    edge_out,
    sems,
):
    n, w = latents.shape
    e = edges.shape[0]
    t = table.shape[0]
    depth = h0.shape[0]
    chunk = e // 2
    total = count_ref[0]
    table[:n] = latents[...]
    odd_s, odd_c = parities()
    for i, (near, far, odd, axis) in enumerate(
        ((h0, h1, odd_s, "stream"), (h2, h3, odd_c, "cross"))
    ):
        place = lax.axis_index(axis)
        a, b = (near[...], far[...])
        zero = jnp.zeros_like(a)
        before = jnp.where(place > 0, jnp.where(odd == 1, a, b), zero)
        after = jnp.where(place < lax.axis_size(axis) - 1, jnp.where(odd == 1, b, a), zero)
        at = n + 2 * i * depth
        table[at : at + depth] = before
        table[at + depth : at + 2 * depth] = after
    gain = edge_gain[...]

    for c in range(e // chunk):
        rows = slice(c * chunk, (c + 1) * chunk)
        for b in range(chunk // w):
            row = c * (chunk // w) + b
            part = slice(row * w, (row + 1) * w)
            column, upper = folded(index_columns(senders, row), t // 2)
            found = mm(one_hot_rows(column, t // 2), side_by_side(table))
            joined[part, :w] = chosen(found, upper).astype(BF)
            upper_send[part] = jnp.where(upper, 1.0, 0.0).astype(BF)
            column, upper = folded(index_columns(receivers, row), n // 2)
            hot = one_hot_rows(column, n // 2)
            hot_recv[part] = hot
            found = mm(hot, side_by_side(latents))
            joined[part, w:] = chosen(found, upper).astype(BF)
            upper_recv[part] = jnp.where(upper, 1.0, 0.0).astype(BF)
            turn_send[:, part] = one_hot_columns(senders, row, t // 2, True)
            turn_recv[:, part] = one_hot_columns(receivers, row, n // 2, True)
        edge = edges[rows]
        pre = mm(edge, edge_first[:w]) + mm(joined[rows], edge_first[w:]) + edge_bias[...]
        hidden, slope = silu_pair(pre)
        hidden = hidden.astype(BF)
        hidden_s[rows] = hidden
        slope_s[rows] = slope
        unit, inverse = norm_forward(mm(hidden, edge_second[...]))
        unit_s[rows] = unit
        inverse_s[rows] = inverse
        place = lax.broadcasted_iota(jnp.int32, (chunk, w), 0) + c * chunk
        fresh = (edge.astype(F32) + unit * gain).astype(BF)
        fresh = jnp.where(place < total, fresh, jnp.zeros_like(fresh))
        alive_edges[rows] = parted(fresh, upper_recv[rows] > 0)

    aggregate = stacked(mm(turn_recv[...], alive_edges[...])).astype(BF)
    own = latents[...]
    hidden, slope = silu_pair(
        mm(jnp.concatenate([own, aggregate], axis=1), node_first[...]) + node_bias[...]
    )
    hidden = hidden.astype(BF)
    unit, inverse = norm_forward(mm(hidden, node_second[...]))
    latent_out[...] = (own.astype(F32) + unit * node_gain[...]).astype(BF)
    send_latents = pltpu.make_async_copy(latent_out, new_latents, sems.at[0])
    send_latents.start()
    ncot = node_cot[...].astype(F32)
    node_gain_grad = jnp.sum(ncot * unit, axis=0, keepdims=True)
    dz = norm_backward(ncot * node_gain[...], unit, inverse).astype(BF)
    dpre = mm_nt(dz, node_second[...]) * slope
    node_bias_grad = jnp.sum(dpre, axis=0, keepdims=True)
    dpre = dpre.astype(BF)
    down = mm_nt(dpre, node_first[...])
    d_aggregate = side_by_side(down[:, w:].astype(BF))
    latent_part = ncot + down[:, :w]
    at = 4 * w
    packed[at : at + w] = mm_tn(own, dpre).astype(BF)
    packed[at + w : at + 2 * w] = mm_tn(aggregate, dpre).astype(BF)
    packed[at + 2 * w : at + 3 * w] = mm_tn(hidden, dz).astype(BF)

    bias_grad = jnp.zeros((1, w), F32)
    gain_grad = jnp.zeros((1, w), F32)
    for c in range(e // chunk):
        rows = slice(c * chunk, (c + 1) * chunk)
        place = lax.broadcasted_iota(jnp.int32, (chunk, w), 0) + c * chunk
        alive = place < total
        upper = upper_recv[rows] > 0
        passed = chosen(mm(hot_recv[rows], d_aggregate), upper)
        cot = edge_cot[rows].astype(F32) + jnp.where(alive, passed, 0.0)
        live = jnp.where(alive, cot, 0.0)
        unit = unit_s[rows]
        gain_grad = gain_grad + jnp.sum(live * unit, axis=0, keepdims=True)
        dz = norm_backward(live * gain, unit, inverse_s[rows]).astype(BF)
        dz_s[rows] = dz
        dpre = mm_nt(dz, edge_second[...]) * slope_s[rows]
        bias_grad = bias_grad + jnp.sum(dpre, axis=0, keepdims=True)
        dpre = dpre.astype(BF)
        dpre_s[rows] = dpre
        dpre_send[rows] = parted(dpre, upper_send[rows] > 0)
        dpre_recv[rows] = parted(dpre, upper)
        edge_out[rows] = (cot + mm_nt(dpre, edge_first[:w])).astype(BF)
    send_edges = pltpu.make_async_copy(edge_out, edge_grads, sems.at[1])
    send_edges.start()

    from_send = stacked(mm(turn_send[...], dpre_send[...])).astype(BF)
    from_recv = stacked(mm(turn_recv[...], dpre_recv[...])).astype(BF)
    back = mm_nt(from_send, edge_first[w : 2 * w])
    grad_out[...] = (latent_part + back[:n] + mm_nt(from_recv, edge_first[2 * w :])).astype(BF)
    send_grads = pltpu.make_async_copy(grad_out, latent_grads, sems.at[2])
    send_grads.start()
    for i, (near, far, odd) in enumerate(((g0, g1, odd_s), (g2, g3, odd_c))):
        at = n + 2 * i * depth
        before = back[at : at + depth]
        after = back[at + depth : at + 2 * depth]
        near[...] = jnp.where(odd == 1, before, after).astype(BF)
        far[...] = jnp.where(odd == 1, after, before).astype(BF)

    dpre = dpre_s[...]
    packed[:w] = mm_tn(edges[...], dpre).astype(BF)
    packed[w : 3 * w] = mm_tn(joined[...], dpre).astype(BF)
    packed[3 * w : 4 * w] = mm_tn(hidden_s[...], dz_s[...]).astype(BF)
    tail = jnp.concatenate(
        [
            bias_grad,
            gain_grad,
            node_bias_grad,
            node_gain_grad,
            jnp.zeros((packed.shape[0] - 7 * w - 4, w), F32),
        ],
        axis=0,
    )
    packed[7 * w :] = tail.astype(BF)
    send_latents.wait()
    send_edges.wait()
    send_grads.wait()


def final_kernel(limit, mine, other, *outs):
    swap = half_of() == 1
    a, b = (mine[...].astype(F32), other[...].astype(F32))
    low = jnp.where(swap, b, a)
    high = jnp.where(swap, a, b)
    squares = jnp.sum(a * a + b * b)
    factor = jnp.minimum(1.0, limit * lax.rsqrt(jnp.full((1, a.shape[1]), squares, F32)))
    full = jnp.concatenate([low, high], axis=0) * factor
    ef, eb, es, eg, nf, nb, ns, ng = outs
    at = 0
    for out in (ef, es, nf, ns, eb, eg, nb, ng):
        out[...] = full[at : at + out.shape[0]]
        at += out.shape[0]


VM = pl.BlockSpec(memory_space=pltpu.VMEM)
SM = pl.BlockSpec(memory_space=pltpu.SMEM)
HB = pl.BlockSpec(memory_space=pltpu.HBM)


def call(kernel, outs, scratch=(), specs=None, out_specs=None):
    return pl.pallas_call(
        kernel,
        out_shape=outs,
        in_specs=specs,
        out_specs=out_specs or jax.tree.map(lambda _: VM, outs),
        scratch_shapes=list(scratch),
        compiler_params=pltpu.CompilerParams(vmem_limit_bytes=VMEM_LIMIT),
    )


def flip(axis, bit):
    return [(i, i ^ bit) for i in range(lax.axis_size(axis))]


def pair_sum(parts):
    parts = [p.astype(F32) for p in parts]
    while len(parts) > 1:
        parts = [parts[i] + parts[i + 1] for i in range(0, len(parts), 2)]
    return parts[0].astype(BF)


def level_flip(mask):
    stream, cross = (lax.axis_size("stream"), lax.axis_size("cross"))
    turn = mask >> 1 & 1
    return [
        (s * cross + c, (s ^ turn) * cross + (c ^ mask)) for s in range(stream) for c in range(cross)
    ]


def level_exchange(value, bits):
    out = [value]
    for m in range(1, 1 << len(bits)):
        mask = sum(bits[j] for j in range(len(bits)) if m >> j & 1)
        out.append(lax.ppermute(value, ("stream", "cross"), level_flip(mask)))
    return out


def exchange(value, axis, bits):
    out = [value]
    for m in range(1, 1 << len(bits)):
        mask = sum(bits[j] for j in range(len(bits)) if m >> j & 1)
        out.append(lax.ppermute(value, axis, flip(axis, mask)))
    return out


def scatter_sum(value, axis, masks, spot):
    radix = len(masks) + 1
    blocks = value.reshape((radix, value.shape[0] // radix) + value.shape[1:])
    got = [lax.dynamic_index_in_dim(blocks, spot, 0, False)]
    for k, mask in enumerate(masks):
        block = lax.dynamic_index_in_dim(blocks, spot ^ (k + 1), 0, False)
        got.append(lax.ppermute(block, axis, flip(axis, mask)))
    return got


def gather_back(value, axis, masks, spot):
    stack = jnp.stack([value] + [lax.ppermute(value, axis, flip(axis, m)) for m in masks])
    return jnp.concatenate(
        [lax.dynamic_index_in_dim(stack, spot ^ k, 0, False) for k in range(len(masks) + 1)],
        axis=0,
    )


QUAD = (3, 4, 7)


def half_of():
    place, level = (lax.axis_index("stream"), lax.axis_index("cross"))
    return lax.rem(place, 2) ^ lax.rem(place // 2, 2) ^ lax.rem(level // 2, 2)


def quarter_of(axis):
    return lax.rem(lax.axis_index(axis) // 2, 4)


def together(first, *rest):
    return lax.optimization_barrier((first,) + rest)


def odd_exchange(value, axis):
    stream, cross = (lax.axis_size("stream"), lax.axis_size("cross"))
    pairs = []
    for s in range(stream):
        for c in range(cross):
            place, size = (s, stream) if axis == "stream" else (c, cross)
            to = place + 1 if place % 2 else place - 1
            if axis == "stream":
                peer = (to, c) if 0 <= to < size else (s, c ^ 1)
            else:
                peer = (s, to) if 0 <= to < size else (s ^ 1, c)
            pairs.append((s * cross + c, peer[0] * cross + peer[1]))
    return lax.ppermute(value, ("stream", "cross"), pairs)


def pair_exchange(near, far, axis):
    return (lax.ppermute(near, axis, flip(axis, 1)), odd_exchange(far, axis))


def reduce_all(value, near_s, far_s, near_c, far_c):
    stream, cross = (lax.axis_size("stream"), lax.axis_size("cross"))
    half, quarter = (half_of(), quarter_of("stream"))
    blocks = value.reshape((2, value.shape[0] // 2, value.shape[1]))
    mine = lax.dynamic_index_in_dim(blocks, half, 0, False)
    give = lax.dynamic_index_in_dim(blocks, 1 - half, 0, False)
    back_c = lax.ppermute(near_c, "cross", flip("cross", 1))
    got = lax.ppermute(jnp.concatenate([give, near_s]), "stream", flip("stream", 1))
    value = pair_sum([mine, got[: mine.shape[0]]])
    back_s = got[mine.shape[0] :]
    value, far_c = together(value, far_c)
    back_d = odd_exchange(far_c, "cross")
    parts, back_c = together(scatter_sum(value, "stream", QUAD, quarter), back_c)
    value = pair_sum(parts)
    low = 8
    while low < stream:
        value = pair_sum(exchange(value, "stream", [low]))
        low *= 2
    value, far_s = together(value, far_s)
    parts = level_exchange(value, [1, 2])
    back_b = odd_exchange(far_s, "stream")
    parts, back_d, back_b = together(parts, back_d, back_b)
    value = pair_sum(parts)
    low = 4
    while low < cross:
        value = pair_sum(level_exchange(value, [low, 2 * low] if 2 * low < cross else [low]))
        low *= 4
    value = gather_back(value, "stream", QUAD, quarter)
    return (value, (back_s, back_b, back_c, back_d))


def per_device(
    latents,
    stale_latents,
    edge_latents,
    senders,
    receivers,
    edge_count,
    send_list,
    node_cotangent,
    edge_cotangent,
    edge_first,
    edge_bias,
    edge_second,
    edge_gain,
    node_first,
    node_bias,
    node_second,
    node_gain,
):
    n, w = latents.shape
    e = edge_latents.shape[0]
    depth = send_list.shape[2]
    lists = send_list[0]

    sources = (
        latents,
        edge_latents,
        senders.reshape(e // w, w),
        receivers.reshape(e // w, w),
        node_cotangent,
        edge_cotangent,
        edge_first,
        edge_bias.reshape(1, w),
        edge_second,
        edge_gain.reshape(1, w),
        node_first,
        node_bias.reshape(1, w),
        node_second,
        node_gain.reshape(1, w),
    )
    loaded = call(
        load_kernel,
        (jax.ShapeDtypeStruct((depth, w), BF),) * 4
        + (jax.ShapeDtypeStruct(lists.shape, lists.dtype),)
        + tuple(jax.ShapeDtypeStruct(x.shape, x.dtype) for x in sources),
        scratch=(
            pltpu.VMEM((n, w), BF),
            pltpu.SemaphoreType.DMA((2 + len(sources),)),
        ),
        specs=[HB] * (2 + len(sources)),
    )(*(pltpu.with_memory_space_constraint(x, pltpu.HBM) for x in (lists, stale_latents) + sources))
    picked, lists, kept = (loaded[:4], loaded[4], loaded[5:])
    halo = pair_exchange(picked[2], picked[3], "cross")
    halo = pair_exchange(picked[0], picked[1], "stream") + halo
    table = n + 4 * depth

    def shape(rows, kind=BF):
        return jax.ShapeDtypeStruct((rows, w), kind)

    new_latents, latent_grads, edge_grads, g0, g1, g2, g3, packed = call(
        main_kernel,
        (shape(n), shape(n), shape(e)) + (shape(depth),) * 4 + (shape(-(-(7 * w + 4) // 64) * 64),),
        scratch=(
            pltpu.VMEM((table, w), BF),
            pltpu.VMEM((e, n // 2), BF),
            pltpu.VMEM((n // 2, e), BF),
            pltpu.VMEM((table // 2, e), BF),
            pltpu.VMEM((e, 2 * w), BF),
            pltpu.VMEM((e, w), BF),
            pltpu.VMEM((e, w), F32),
            pltpu.VMEM((e, w), F32),
            pltpu.VMEM((e, w), F32),
            pltpu.VMEM((e, w), BF),
            pltpu.VMEM((e, w), BF),
            pltpu.VMEM((e, 2 * w), BF),
            pltpu.VMEM((e, w), BF),
            pltpu.VMEM((e, w), BF),
            pltpu.VMEM((e, 2 * w), BF),
            pltpu.VMEM((e, 2 * w), BF),
            pltpu.VMEM((n, w), BF),
            pltpu.VMEM((n, w), BF),
            pltpu.VMEM((e, w), BF),
            pltpu.SemaphoreType.DMA((3,)),
        ),
        specs=[SM] + [VM] * 18,
        out_specs=(HB,) * 3 + (VM,) * 5,
    )(
        edge_count, kept[0], *halo, *kept[1:]
    )
    part, returned = reduce_all(packed, g0, g1, g2, g3)
    stale_grads = call(stale_kernel, shape(n), specs=[VM] * 5)(lists, *returned)
    other = lax.ppermute(part, "stream", flip("stream", 1))
    sizes = (3 * w * w, w, w * w, w, 2 * w * w, w, w * w, w)
    limit = math.sqrt(sum(sizes))
    clipped = call(
        functools.partial(final_kernel, limit),
        tuple(shape(s // w, F32) for s in sizes),
        specs=[VM, VM],
    )(part, other)
    clipped = tuple(c.reshape(w) if s == w else c for c, s in zip(clipped, sizes))
    return (new_latents, latent_grads, stale_grads, edge_grads) + clipped


def solution(mesh):
    shard = P(("stream", "cross"))
    rows = P(("stream", "cross"), None)
    in_specs = (rows, rows, rows, shard, shard, shard, P(("stream", "cross"), None, None), rows, rows)
    in_specs = in_specs + (P(),) * 8
    out_specs = (rows,) * 4 + (P(),) * 8
    return jax.shard_map(
        per_device, mesh=mesh, in_specs=in_specs, out_specs=out_specs, check_vma=False
    )
```

profile of v0, /device:TPU:1, one launch (start us, length us, event | category | flops | bytes accessed | tf_op | source)
XLA Modules:
  0.0 40.9 jit_solution(18417753915494010180)
XLA Ops:
  0.7 1.5 %shard_map.256 = (bf16[128,128]{1,0:T(8,128)(2,1)S(1)}, bf16[128,128]{1,0:T(8,128)(2,1)S(1)}, bf16[128,128]{1,0:T(8,128)(2,1)S(1)}, bf16[128,128]{1,0:T(8,128)(2...) custom-call(s32[4,128]{1,0:T(4,128)} %bitcast.47, ...), custom_call_target="tpu_custom_call" | custom-call | tf_op jit(solution)/shard_map/pallas_call | solution.py:531
  2.2 0.1 collective-permute-start
  2.3 2.6 %collective-permute-start.1 = (bf16[128,128]{1,0:T(8,128)(2,1)S(1)}, bf16[128,128]{1,0:T(8,128)(2,1)S(1)}, u32[]{:S(2)}, u32[]{:S(2)}) collective-permute-start(bf16[128,128]{1,0:T(8,128)(2,1)S(1)} %get-tuple-element.64), channel_id=1, source_target_pairs={{0,1},{1,0},{2,3},{3,2},{4,8},{5,9},{6,10},{7,11},{8,4},{9,5},{10,... | collective-permute-start | bytes 98312 | tf_op jit(solution)/shard_map/ppermute | solution.py:453
  4.9 1.3 %collective-permute-start.2 = (bf16[128,128]{1,0:T(8,128)(2,1)S(1)}, bf16[128,128]{1,0:T(8,128)(2,1)S(1)}, u32[]{:S(2)}, u32[]{:S(2)}) collective-permute-start(bf16[128,128]{1,0:T(8,128)(2,1)S(1)} %get-tuple-element.65), channel_id=1, source_target_pairs={{0,1},{1,0},{2,3},{3,2},{4,5},{5,4},{6,7},{7,6},{8,9},{9,8},{10,11... | collective-permute-start | bytes 98312 | tf_op jit(solution)/shard_map/ppermute | solution.py:457
  6.2 0.0 collective-permute-start.3
  6.9 0.0 collective-permute-done.h0
  6.9 0.0 collective-permute-done.1.h1
  6.9 0.8 %collective-permute-done.2.h2 = bf16[128,128]{1,0:T(8,128)(2,1)S(1)} collective-permute-done((bf16[128,128]{1,0:T(8,128)(2,1)S(1)}, bf16[128,128]{1,0:T(8,128)(2,1)S(1)}, u32[]{:S(2)}, u32[]{:S(2)}) %collective-permute-start.2) | collective-permute-done | bytes 32800 | tf_op jit(solution)/shard_map/ppermute | solution.py:457
  7.7 0.0 collective-permute-done.3.h3
  7.7 5.7 %shard_map.257 = (bf16[512,128]{1,0:T(8,128)(2,1)}, bf16[512,128]{1,0:T(8,128)(2,1)}, bf16[1536,128]{1,0:T(8,128)(2,1)}, bf16[128,128]{1,0:T(8,128)(2,1)S(1)}, b...) custom-call(s32[1]{0:T(128)S(6)} %copy.29.count_ref, ...), custom_call_target="tpu_custom_call" | custom-call | tf_op jit(solution)/shard_map/pallas_call | solution.py:550
  13.5 1.7 %collective-permute-start.4 = (bf16[608,128]{1,0:T(8,128)(2,1)S(1)}, bf16[608,128]{1,0:T(8,128)(2,1)S(1)}, u32[]{:S(2)}, u32[]{:S(2)}) collective-permute-start(bf16[608,128]{1,0:T(8,128)(2,1)S(1)} %pad_maximum_fusion), channel_id=1, source_target_pairs={{0,4},{4,0},{8,12},{12,8},{16,20},{20,16},{24,28},{28,24},{1,5},{5... | collective-permute-start | bytes 466952 | tf_op jit(solution)/shard_map/ppermute | solution.py:467
  15.2 1.8 %collective-permute-start.8 = (bf16[128,128]{1,0:T(8,128)(2,1)S(1)}, bf16[128,128]{1,0:T(8,128)(2,1)S(1)}, u32[]{:S(2)}, u32[]{:S(2)}) collective-permute-start(bf16[128,128]{1,0:T(8,128)(2,1)S(1)} %get-tuple-element.87), channel_id=1, source_target_pairs={{0,1},{1,0},{2,3},{3,2},{4,5},{5,4},{6,7},{7,6},{8,9},{9,8},{10,11... | collective-permute-start | bytes 98312 | tf_op jit(solution)/shard_map/ppermute | solution.py:466
  17.0 0.0 collective-permute-done.4
  17.1 1.4 %collective-permute-start.5 = (bf16[120,128]{1,0:T(8,128)(2,1)S(1)}, bf16[120,128]{1,0:T(8,128)(2,1)S(1)}, u32[]{:S(2)}, u32[]{:S(2)}) collective-permute-start(bf16[120,128]{1,0:T(8,128)(2,1)S(1)} %get-tuple-element.118), channel_id=1, source_target_pairs={{0,12},{4,8},{8,4},{12,0},{16,28},{20,24},{24,20},{28,16},{1,13},{... | collective-permute-start | bytes 92168 | tf_op jit(solution)/shard_map/ppermute | solution.py:413
  18.5 1.0 %collective-permute-start.6 = (bf16[120,128]{1,0:T(8,128)(2,1)S(1)}, bf16[120,128]{1,0:T(8,128)(2,1)S(1)}, u32[]{:S(2)}, u32[]{:S(2)}) collective-permute-start(bf16[120,128]{1,0:T(8,128)(2,1)S(1)} %get-tuple-element.117), channel_id=1, source_target_pairs={{0,16},{4,20},{8,24},{12,28},{16,0},{20,4},{24,8},{28,12},{1,17},{... | collective-permute-start | bytes 92168 | tf_op jit(solution)/shard_map/ppermute | solution.py:413
  19.5 0.9 %collective-permute-start.7 = (bf16[120,128]{1,0:T(8,128)(2,1)S(1)}, bf16[120,128]{1,0:T(8,128)(2,1)S(1)}, u32[]{:S(2)}, u32[]{:S(2)}) collective-permute-start(bf16[120,128]{1,0:T(8,128)(2,1)S(1)} %get-tuple-element.116), channel_id=1, source_target_pairs={{0,28},{4,24},{8,20},{12,16},{16,12},{20,8},{24,4},{28,0},{1,29},{... | collective-permute-start | bytes 92168 | tf_op jit(solution)/shard_map/ppermute | solution.py:413
  20.3 0.4 collective-permute-start.12
  20.7 0.0 collective-permute-done.8.b2
  20.7 0.0 collective-permute-done.5
  20.7 0.5 %collective-permute-done.6 = bf16[120,128]{1,0:T(8,128)(2,1)S(1)} collective-permute-done((bf16[120,128]{1,0:T(8,128)(2,1)S(1)}, bf16[120,128]{1,0:T(8,128)(2,1)S(1)}, u32[]{:S(2)}, u32[]{:S(2)}) %collective-permute-start.6) | collective-permute-done | bytes 30752 | tf_op jit(solution)/shard_map/ppermute | solution.py:413
  21.2 2.5 %collective-permute-done.7 = bf16[120,128]{1,0:T(8,128)(2,1)S(1)} collective-permute-done((bf16[120,128]{1,0:T(8,128)(2,1)S(1)}, bf16[120,128]{1,0:T(8,128)(2,1)S(1)}, u32[]{:S(2)}, u32[]{:S(2)}) %collective-permute-start.7) | collective-permute-done | bytes 30752 | tf_op jit(solution)/shard_map/ppermute | solution.py:413
  23.7 1.5 %collective-permute-start.13 = (bf16[128,128]{1,0:T(8,128)(2,1)S(1)}, bf16[128,128]{1,0:T(8,128)(2,1)S(1)}, u32[]{:S(2)}, u32[]{:S(2)}) collective-permute-start(bf16[128,128]{1,0:T(8,128)(2,1)S(1)} %get-tuple-element.95), channel_id=1, source_target_pairs={{0,1},{1,0},{2,3},{3,2},{4,8},{5,9},{6,10},{7,11},{8,4},{9,5},{10,... | collective-permute-start | bytes 98312 | tf_op jit(solution)/shard_map/ppermute | solution.py:453
  25.2 2.0 %collective-permute-start.10 = (bf16[120,128]{1,0:T(8,128)(2,1)S(1)}, bf16[120,128]{1,0:T(8,128)(2,1)S(1)}, u32[]{:S(2)}, u32[]{:S(2)}) collective-permute-start(bf16[120,128]{1,0:T(8,128)(2,1)S(1)} %add_convert_fusion.1), channel_id=1, source_target_pairs={{0,6},{1,7},{2,4},{3,5},{4,2},{5,3},{6,0},{7,1},{8,14},{9,15},{10,... | collective-permute-start | bytes 92168 | tf_op jit(solution)/shard_map/ppermute | solution.py:395
  27.3 1.4 %collective-permute-start.11 = (bf16[120,128]{1,0:T(8,128)(2,1)S(1)}, bf16[120,128]{1,0:T(8,128)(2,1)S(1)}, u32[]{:S(2)}, u32[]{:S(2)}) collective-permute-start(bf16[120,128]{1,0:T(8,128)(2,1)S(1)} %add_convert_fusion.1), channel_id=1, source_target_pairs={{0,7},{1,6},{2,5},{3,4},{4,3},{5,2},{6,1},{7,0},{8,15},{9,14},{10,... | collective-permute-start | bytes 92168 | tf_op jit(solution)/shard_map/ppermute | solution.py:395
  28.6 0.0 collective-permute-start.9
  28.6 0.0 collective-permute-done.12.b3
  28.6 1.1 %collective-permute-done.10 = bf16[120,128]{1,0:T(8,128)(2,1)S(1)} collective-permute-done((bf16[120,128]{1,0:T(8,128)(2,1)S(1)}, bf16[120,128]{1,0:T(8,128)(2,1)S(1)}, u32[]{:S(2)}, u32[]{:S(2)}) %collective-permute-start.10) | collective-permute-done | bytes 30752 | tf_op jit(solution)/shard_map/ppermute | solution.py:395
  29.8 3.1 %collective-permute-done.11 = bf16[120,128]{1,0:T(8,128)(2,1)S(1)} collective-permute-done((bf16[120,128]{1,0:T(8,128)(2,1)S(1)}, bf16[120,128]{1,0:T(8,128)(2,1)S(1)}, u32[]{:S(2)}, u32[]{:S(2)}) %collective-permute-start.11) | collective-permute-done | bytes 30752 | tf_op jit(solution)/shard_map/ppermute | solution.py:395
  32.9 0.0 collective-permute-done.9
  32.9 0.0 collective-permute-done.13.b1
  32.9 0.8 %collective-permute-start.14 = (bf16[120,128]{1,0:T(8,128)(2,1)S(1)}, bf16[120,128]{1,0:T(8,128)(2,1)S(1)}, u32[]{:S(2)}, u32[]{:S(2)}) collective-permute-start(bf16[120,128]{1,0:T(8,128)(2,1)S(1)} %add_convert_fusion), channel_id=1, source_target_pairs={{0,12},{4,8},{8,4},{12,0},{16,28},{20,24},{24,20},{28,16},{1,13},{... | collective-permute-start | bytes 92168 | tf_op jit(solution)/shard_map/ppermute | solution.py:418
  33.7 0.5 %collective-permute-start.15 = (bf16[120,128]{1,0:T(8,128)(2,1)S(1)}, bf16[120,128]{1,0:T(8,128)(2,1)S(1)}, u32[]{:S(2)}, u32[]{:S(2)}) collective-permute-start(bf16[120,128]{1,0:T(8,128)(2,1)S(1)} %add_convert_fusion), channel_id=1, source_target_pairs={{0,16},{4,20},{8,24},{12,28},{16,0},{20,4},{24,8},{28,12},{1,17},{... | collective-permute-start | bytes 92168 | tf_op jit(solution)/shard_map/ppermute | solution.py:418
  34.2 2.0 %collective-permute-start.16 = (bf16[120,128]{1,0:T(8,128)(2,1)S(1)}, bf16[120,128]{1,0:T(8,128)(2,1)S(1)}, u32[]{:S(2)}, u32[]{:S(2)}) collective-permute-start(bf16[120,128]{1,0:T(8,128)(2,1)S(1)} %add_convert_fusion), channel_id=1, source_target_pairs={{0,28},{4,24},{8,20},{12,16},{16,12},{20,8},{24,4},{28,0},{1,29},{... | collective-permute-start | bytes 92168 | tf_op jit(solution)/shard_map/ppermute | solution.py:418
  36.2 0.7 %collective-permute-done.14 = bf16[120,128]{1,0:T(8,128)(2,1)S(1)} collective-permute-done((bf16[120,128]{1,0:T(8,128)(2,1)S(1)}, bf16[120,128]{1,0:T(8,128)(2,1)S(1)}, u32[]{:S(2)}, u32[]{:S(2)}) %collective-permute-start.14) | collective-permute-done | bytes 30752 | tf_op jit(solution)/shard_map/ppermute | solution.py:418
  36.9 0.0 collective-permute-done.15
  36.9 1.5 %collective-permute-done.16 = bf16[120,128]{1,0:T(8,128)(2,1)S(1)} collective-permute-done((bf16[120,128]{1,0:T(8,128)(2,1)S(1)}, bf16[120,128]{1,0:T(8,128)(2,1)S(1)}, u32[]{:S(2)}, u32[]{:S(2)}) %collective-permute-start.16) | collective-permute-done | bytes 30752 | tf_op jit(solution)/shard_map/ppermute | solution.py:418
  38.5 0.2 collective-permute-start.17
  38.7 0.9 %shard_map.258 = bf16[512,128]{1,0:T(8,128)(2,1)} custom-call(s32[4,128]{1,0:T(4,128)S(1)} %get-tuple-element.82.list_ref, bf16[128,128]{1,0:T(8,128)(2,1)S(1)} %slice.8.b0, bf16[128,128]{1,0:T(8,128)(2,1)S(1)} %collective-permute-done.13.b1, bf16[128,128]{1,0:T(8,128)(2,1)S(1)} %collective-permute-done.8.b2, bf16[128,128]{1,0:T(8,128)(2,1)S(1)} %collective-permute-done.12.b3), custom_call_target="tpu_custom_call" | custom-call | tf_op jit(solution)/shard_map/pallas_call | solution.py:581
  39.6 0.3 collective-permute-done.17.other
  39.9 1.0 %shard_map.259 = (f32[384,128]{1,0:T(8,128)}, f32[1,128]{1,0:T(1,128)}, f32[128,128]{1,0:T(8,128)}, f32[1,128]{1,0:T(1,128)}, f32[256,128]{1,0:T(8,128)}, /*inde...) custom-call(bf16[480,128]{1,0:T(8,128)(2,1)S(1)} %pad_maximum_fusion.2.mine, ...), custom_call_target="tpu_custom_call" | custom-call | tf_op jit(solution)/shard_map/pallas_call | solution.py:585
  (10 shorter events, 0.2 us)
Async XLA Ops:
  2.2 4.7 %collective-permute-start = (bf16[128,128]{1,0:T(8,128)(2,1)S(1)}, bf16[128,128]{1,0:T(8,128)(2,1)S(1)}, u32[]{:S(2)}, u32[]{:S(2)}) collective-permute-start(bf16[128,128]{1,0:T(8,128)(2,1)S(1)} %get-tuple-element.63), channel_id=1, source_target_pairs={{0,4},{4,0},{8,12},{12,8},{16,20},{20,16},{24,28},{28,24},{1,5},{5... | collective-permute-start | bytes 98312 | tf_op jit(solution)/shard_map/ppermute | solution.py:457
  2.3 4.6 %collective-permute-start.1 = (bf16[128,128]{1,0:T(8,128)(2,1)S(1)}, bf16[128,128]{1,0:T(8,128)(2,1)S(1)}, u32[]{:S(2)}, u32[]{:S(2)}) collective-permute-start(bf16[128,128]{1,0:T(8,128)(2,1)S(1)} %get-tuple-element.64), channel_id=1, source_target_pairs={{0,1},{1,0},{2,3},{3,2},{4,8},{5,9},{6,10},{7,11},{8,4},{9,5},{10,... | collective-permute-start | bytes 98312 | tf_op jit(solution)/shard_map/ppermute | solution.py:453
  4.9 2.8 %collective-permute-start.2 = (bf16[128,128]{1,0:T(8,128)(2,1)S(1)}, bf16[128,128]{1,0:T(8,128)(2,1)S(1)}, u32[]{:S(2)}, u32[]{:S(2)}) collective-permute-start(bf16[128,128]{1,0:T(8,128)(2,1)S(1)} %get-tuple-element.65), channel_id=1, source_target_pairs={{0,1},{1,0},{2,3},{3,2},{4,5},{5,4},{6,7},{7,6},{8,9},{9,8},{10,11... | collective-permute-start | bytes 98312 | tf_op jit(solution)/shard_map/ppermute | solution.py:457
  6.2 1.5 %collective-permute-start.3 = (bf16[128,128]{1,0:T(8,128)(2,1)S(1)}, bf16[128,128]{1,0:T(8,128)(2,1)S(1)}, u32[]{:S(2)}, u32[]{:S(2)}) collective-permute-start(bf16[128,128]{1,0:T(8,128)(2,1)S(1)} %get-tuple-element.66), channel_id=1, source_target_pairs={{0,4},{1,2},{2,1},{3,7},{4,0},{5,6},{6,5},{7,3},{8,12},{9,10},{10,... | collective-permute-start | bytes 98312 | tf_op jit(solution)/shard_map/ppermute | solution.py:453
  13.5 3.5 %collective-permute-start.4 = (bf16[608,128]{1,0:T(8,128)(2,1)S(1)}, bf16[608,128]{1,0:T(8,128)(2,1)S(1)}, u32[]{:S(2)}, u32[]{:S(2)}) collective-permute-start(bf16[608,128]{1,0:T(8,128)(2,1)S(1)} %pad_maximum_fusion), channel_id=1, source_target_pairs={{0,4},{4,0},{8,12},{12,8},{16,20},{20,16},{24,28},{28,24},{1,5},{5... | collective-permute-start | bytes 466952 | tf_op jit(solution)/shard_map/ppermute | solution.py:467
  15.2 5.6 %collective-permute-start.8 = (bf16[128,128]{1,0:T(8,128)(2,1)S(1)}, bf16[128,128]{1,0:T(8,128)(2,1)S(1)}, u32[]{:S(2)}, u32[]{:S(2)}) collective-permute-start(bf16[128,128]{1,0:T(8,128)(2,1)S(1)} %get-tuple-element.87), channel_id=1, source_target_pairs={{0,1},{1,0},{2,3},{3,2},{4,5},{5,4},{6,7},{7,6},{8,9},{9,8},{10,11... | collective-permute-start | bytes 98312 | tf_op jit(solution)/shard_map/ppermute | solution.py:466
  17.1 3.7 %collective-permute-start.5 = (bf16[120,128]{1,0:T(8,128)(2,1)S(1)}, bf16[120,128]{1,0:T(8,128)(2,1)S(1)}, u32[]{:S(2)}, u32[]{:S(2)}) collective-permute-start(bf16[120,128]{1,0:T(8,128)(2,1)S(1)} %get-tuple-element.118), channel_id=1, source_target_pairs={{0,12},{4,8},{8,4},{12,0},{16,28},{20,24},{24,20},{28,16},{1,13},{... | collective-permute-start | bytes 92168 | tf_op jit(solution)/shard_map/ppermute | solution.py:413
  18.5 2.7 %collective-permute-start.6 = (bf16[120,128]{1,0:T(8,128)(2,1)S(1)}, bf16[120,128]{1,0:T(8,128)(2,1)S(1)}, u32[]{:S(2)}, u32[]{:S(2)}) collective-permute-start(bf16[120,128]{1,0:T(8,128)(2,1)S(1)} %get-tuple-element.117), channel_id=1, source_target_pairs={{0,16},{4,20},{8,24},{12,28},{16,0},{20,4},{24,8},{28,12},{1,17},{... | collective-permute-start | bytes 92168 | tf_op jit(solution)/shard_map/ppermute | solution.py:413
  19.5 4.2 %collective-permute-start.7 = (bf16[120,128]{1,0:T(8,128)(2,1)S(1)}, bf16[120,128]{1,0:T(8,128)(2,1)S(1)}, u32[]{:S(2)}, u32[]{:S(2)}) collective-permute-start(bf16[120,128]{1,0:T(8,128)(2,1)S(1)} %get-tuple-element.116), channel_id=1, source_target_pairs={{0,28},{4,24},{8,20},{12,16},{16,12},{20,8},{24,4},{28,0},{1,29},{... | collective-permute-start | bytes 92168 | tf_op jit(solution)/shard_map/ppermute | solution.py:413
  20.3 8.3 %collective-permute-start.12 = (bf16[128,128]{1,0:T(8,128)(2,1)S(1)}, bf16[128,128]{1,0:T(8,128)(2,1)S(1)}, u32[]{:S(2)}, u32[]{:S(2)}) collective-permute-start(bf16[128,128]{1,0:T(8,128)(2,1)S(1)} %get-tuple-element.94), channel_id=1, source_target_pairs={{0,4},{1,2},{2,1},{3,7},{4,0},{5,6},{6,5},{7,3},{8,12},{9,10},{10,... | collective-permute-start | bytes 98312 | tf_op jit(solution)/shard_map/ppermute | solution.py:453
  23.7 9.1 %collective-permute-start.13 = (bf16[128,128]{1,0:T(8,128)(2,1)S(1)}, bf16[128,128]{1,0:T(8,128)(2,1)S(1)}, u32[]{:S(2)}, u32[]{:S(2)}) collective-permute-start(bf16[128,128]{1,0:T(8,128)(2,1)S(1)} %get-tuple-element.95), channel_id=1, source_target_pairs={{0,1},{1,0},{2,3},{3,2},{4,8},{5,9},{6,10},{7,11},{8,4},{9,5},{10,... | collective-permute-start | bytes 98312 | tf_op jit(solution)/shard_map/ppermute | solution.py:453
  25.2 4.5 %collective-permute-start.10 = (bf16[120,128]{1,0:T(8,128)(2,1)S(1)}, bf16[120,128]{1,0:T(8,128)(2,1)S(1)}, u32[]{:S(2)}, u32[]{:S(2)}) collective-permute-start(bf16[120,128]{1,0:T(8,128)(2,1)S(1)} %add_convert_fusion.1), channel_id=1, source_target_pairs={{0,6},{1,7},{2,4},{3,5},{4,2},{5,3},{6,0},{7,1},{8,14},{9,15},{10,... | collective-permute-start | bytes 92168 | tf_op jit(solution)/shard_map/ppermute | solution.py:395
  27.3 5.6 %collective-permute-start.11 = (bf16[120,128]{1,0:T(8,128)(2,1)S(1)}, bf16[120,128]{1,0:T(8,128)(2,1)S(1)}, u32[]{:S(2)}, u32[]{:S(2)}) collective-permute-start(bf16[120,128]{1,0:T(8,128)(2,1)S(1)} %add_convert_fusion.1), channel_id=1, source_target_pairs={{0,7},{1,6},{2,5},{3,4},{4,3},{5,2},{6,1},{7,0},{8,15},{9,14},{10,... | collective-permute-start | bytes 92168 | tf_op jit(solution)/shard_map/ppermute | solution.py:395
  28.6 4.2 %collective-permute-start.9 = (bf16[120,128]{1,0:T(8,128)(2,1)S(1)}, bf16[120,128]{1,0:T(8,128)(2,1)S(1)}, u32[]{:S(2)}, u32[]{:S(2)}) collective-permute-start(bf16[120,128]{1,0:T(8,128)(2,1)S(1)} %add_convert_fusion.1), channel_id=1, source_target_pairs={{0,1},{1,0},{2,3},{3,2},{4,5},{5,4},{6,7},{7,6},{8,9},{9,8},{10,11... | collective-permute-start | bytes 92168 | tf_op jit(solution)/shard_map/ppermute | solution.py:395
  32.9 4.0 %collective-permute-start.14 = (bf16[120,128]{1,0:T(8,128)(2,1)S(1)}, bf16[120,128]{1,0:T(8,128)(2,1)S(1)}, u32[]{:S(2)}, u32[]{:S(2)}) collective-permute-start(bf16[120,128]{1,0:T(8,128)(2,1)S(1)} %add_convert_fusion), channel_id=1, source_target_pairs={{0,12},{4,8},{8,4},{12,0},{16,28},{20,24},{24,20},{28,16},{1,13},{... | collective-permute-start | bytes 92168 | tf_op jit(solution)/shard_map/ppermute | solution.py:418
  33.7 3.2 %collective-permute-start.15 = (bf16[120,128]{1,0:T(8,128)(2,1)S(1)}, bf16[120,128]{1,0:T(8,128)(2,1)S(1)}, u32[]{:S(2)}, u32[]{:S(2)}) collective-permute-start(bf16[120,128]{1,0:T(8,128)(2,1)S(1)} %add_convert_fusion), channel_id=1, source_target_pairs={{0,16},{4,20},{8,24},{12,28},{16,0},{20,4},{24,8},{28,12},{1,17},{... | collective-permute-start | bytes 92168 | tf_op jit(solution)/shard_map/ppermute | solution.py:418
  34.2 4.2 %collective-permute-start.16 = (bf16[120,128]{1,0:T(8,128)(2,1)S(1)}, bf16[120,128]{1,0:T(8,128)(2,1)S(1)}, u32[]{:S(2)}, u32[]{:S(2)}) collective-permute-start(bf16[120,128]{1,0:T(8,128)(2,1)S(1)} %add_convert_fusion), channel_id=1, source_target_pairs={{0,28},{4,24},{8,20},{12,16},{16,12},{20,8},{24,4},{28,0},{1,29},{... | collective-permute-start | bytes 92168 | tf_op jit(solution)/shard_map/ppermute | solution.py:418
  38.5 1.4 %collective-permute-start.17 = (bf16[480,128]{1,0:T(8,128)(2,1)S(1)}, bf16[480,128]{1,0:T(8,128)(2,1)S(1)}, u32[]{:S(2)}, u32[]{:S(2)}) collective-permute-start(bf16[480,128]{1,0:T(8,128)(2,1)S(1)} %pad_maximum_fusion.2.mine), channel_id=1, source_target_pairs={{0,4},{4,0},{8,12},{12,8},{16,20},{20,16},{24,28},{28,24},{1,5},{5... | collective-permute-start | bytes 368648 | tf_op jit(solution)/shard_map/ppermute | solution.py:582
where the time goes:
time: 41.2 us; the launch traced here: 40.9 us
  starting transfers between devices  19.5 us (47%)
  waiting for transfers between devices  10.5 us (25%)
  Pallas kernels  9.2 us (22%)
  between operations  1.42 us (3%)
    pallas_call x1, Pallas kernels, per_device(): call(main_kernel, (shape(n), shape(n), shape(e)) + (shape(depth),) * 4 +...  5.73 us
    ppermute x4, starting transfers between devices, odd_exchange(): return lax.ppermute(value, ('stream', 'cross'), pairs)  4.53 us
    ppermute x3, waiting for transfers between devices, level_exchange(): out.append(lax.ppermute(value, ('stream', 'cross'), level_flip(mask)))  4.22 us
    ppermute x3, starting transfers between devices, level_exchange(): out.append(lax.ppermute(value, ('stream', 'cross'), level_flip(mask)))  3.41 us
    ppermute x3, starting transfers between devices, scatter_sum(): got.append(lax.ppermute(block, axis, flip(axis, mask)))  3.27 us
    ppermute x3, starting transfers between devices, gather_back(): lax.ppermute(value, axis, flip(axis, m))  3.27 us
    ppermute x3, waiting for transfers between devices, scatter_sum(): got.append(lax.ppermute(block, axis, flip(axis, mask)))  2.98 us
    ppermute x3, waiting for transfers between devices, gather_back(): lax.ppermute(value, axis, flip(axis, m))  2.25 us
  transfers between devices with their start and end apart: 18, of which 8 were waited for; matrix products, arithmetic and copies ran while one was open for 0% of the time, Pallas kernels for 2%

commit v1 on v0

--- a/solution.py
+++ b/solution.py
@@ -453,10 +453,6 @@
     return lax.ppermute(value, ("stream", "cross"), pairs)
 
 
-def pair_exchange(near, far, axis):
-    return (lax.ppermute(near, axis, flip(axis, 1)), odd_exchange(far, axis))
-
-
 def reduce_all(value, near_s, far_s, near_c, far_c):
     stream, cross = (lax.axis_size("stream"), lax.axis_size("cross"))
     half, quarter = (half_of(), quarter_of("stream"))
@@ -540,8 +536,11 @@
         specs=[HB] * (2 + len(sources)),
     )(*(pltpu.with_memory_space_constraint(x, pltpu.HBM) for x in (lists, stale_latents) + sources))
     picked, lists, kept = (loaded[:4], loaded[4], loaded[5:])
-    halo = pair_exchange(picked[2], picked[3], "cross")
-    halo = pair_exchange(picked[0], picked[1], "stream") + halo
+    near_s = lax.ppermute(picked[0], "stream", flip("stream", 1))
+    far_s = odd_exchange(picked[1], "stream")
+    near_c = lax.ppermute(picked[2], "cross", flip("cross", 1))
+    far_c = odd_exchange(picked[3], "cross")
+    halo = (near_s, far_s, near_c, far_c)
     table = n + 4 * depth
 
     def shape(rows, kind=BF):

time: 41.2 us -> 41.2 us (level)
  no operation moved by 1% of the time
where the time goes in v1:
time: 41.2 us; the launch traced here: 40.9 us
  starting transfers between devices  19.5 us (47%)
  waiting for transfers between devices  10.5 us (25%)
  Pallas kernels  9.2 us (22%)
  between operations  1.42 us (3%)
    pallas_call x1, Pallas kernels, per_device(): call(main_kernel, (shape(n), shape(n), shape(e)) + (shape(depth),) * 4 +...  5.73 us
    ppermute x4, starting transfers between devices, odd_exchange(): return lax.ppermute(value, ('stream', 'cross'), pairs)  4.53 us
    ppermute x3, waiting for transfers between devices, level_exchange(): out.append(lax.ppermute(value, ('stream', 'cross'), level_flip(mask)))  4.22 us
    ppermute x3, starting transfers between devices, level_exchange(): out.append(lax.ppermute(value, ('stream', 'cross'), level_flip(mask)))  3.41 us
    ppermute x3, starting transfers between devices, scatter_sum(): got.append(lax.ppermute(block, axis, flip(axis, mask)))  3.27 us
    ppermute x3, starting transfers between devices, gather_back(): lax.ppermute(value, axis, flip(axis, m))  3.27 us
    ppermute x3, waiting for transfers between devices, scatter_sum(): got.append(lax.ppermute(block, axis, flip(axis, mask)))  2.98 us
    ppermute x3, waiting for transfers between devices, gather_back(): lax.ppermute(value, axis, flip(axis, m))  2.25 us
  transfers between devices with their start and end apart: 18, of which 8 were waited for; matrix products, arithmetic and copies ran while one was open for 0% of the time, Pallas kernels for 2%

profile of v1, /device:TPU:1, one launch (start us, length us, event | category | flops | bytes accessed | tf_op | source)
XLA Modules:
  0.0 40.9 jit_solution(18417753915494010180)
XLA Ops:
  0.7 1.5 %shard_map.256 = (bf16[128,128]{1,0:T(8,128)(2,1)S(1)}, bf16[128,128]{1,0:T(8,128)(2,1)S(1)}, bf16[128,128]{1,0:T(8,128)(2,1)S(1)}, bf16[128,128]{1,0:T(8,128)(2...) custom-call(s32[4,128]{1,0:T(4,128)} %bitcast.47, ...), custom_call_target="tpu_custom_call" | custom-call | tf_op jit(solution)/shard_map/pallas_call | solution.py:527
  2.2 0.1 collective-permute-start
  2.3 2.6 %collective-permute-start.1 = (bf16[128,128]{1,0:T(8,128)(2,1)S(1)}, bf16[128,128]{1,0:T(8,128)(2,1)S(1)}, u32[]{:S(2)}, u32[]{:S(2)}) collective-permute-start(bf16[128,128]{1,0:T(8,128)(2,1)S(1)} %get-tuple-element.64), channel_id=1, source_target_pairs={{0,1},{1,0},{2,3},{3,2},{4,8},{5,9},{6,10},{7,11},{8,4},{9,5},{10,... | collective-permute-start | bytes 98312 | tf_op jit(solution)/shard_map/ppermute | solution.py:453
  4.9 1.3 %collective-permute-start.2 = (bf16[128,128]{1,0:T(8,128)(2,1)S(1)}, bf16[128,128]{1,0:T(8,128)(2,1)S(1)}, u32[]{:S(2)}, u32[]{:S(2)}) collective-permute-start(bf16[128,128]{1,0:T(8,128)(2,1)S(1)} %get-tuple-element.65), channel_id=1, source_target_pairs={{0,1},{1,0},{2,3},{3,2},{4,5},{5,4},{6,7},{7,6},{8,9},{9,8},{10,11... | collective-permute-start | bytes 98312 | tf_op jit(solution)/shard_map/ppermute | solution.py:541
  6.2 0.0 collective-permute-start.3
  6.9 0.0 collective-permute-done.h0
  6.9 0.0 collective-permute-done.1.h1
  6.9 0.8 %collective-permute-done.2.h2 = bf16[128,128]{1,0:T(8,128)(2,1)S(1)} collective-permute-done((bf16[128,128]{1,0:T(8,128)(2,1)S(1)}, bf16[128,128]{1,0:T(8,128)(2,1)S(1)}, u32[]{:S(2)}, u32[]{:S(2)}) %collective-permute-start.2) | collective-permute-done | bytes 32800 | tf_op jit(solution)/shard_map/ppermute | solution.py:541
  7.7 0.0 collective-permute-done.3.h3
  7.7 5.7 %shard_map.257 = (bf16[512,128]{1,0:T(8,128)(2,1)}, bf16[512,128]{1,0:T(8,128)(2,1)}, bf16[1536,128]{1,0:T(8,128)(2,1)}, bf16[128,128]{1,0:T(8,128)(2,1)S(1)}, b...) custom-call(s32[1]{0:T(128)S(6)} %copy.29.count_ref, ...), custom_call_target="tpu_custom_call" | custom-call | tf_op jit(solution)/shard_map/pallas_call | solution.py:549
  13.5 1.7 %collective-permute-start.4 = (bf16[608,128]{1,0:T(8,128)(2,1)S(1)}, bf16[608,128]{1,0:T(8,128)(2,1)S(1)}, u32[]{:S(2)}, u32[]{:S(2)}) collective-permute-start(bf16[608,128]{1,0:T(8,128)(2,1)S(1)} %pad_maximum_fusion), channel_id=1, source_target_pairs={{0,4},{4,0},{8,12},{12,8},{16,20},{20,16},{24,28},{28,24},{1,5},{5... | collective-permute-start | bytes 466952 | tf_op jit(solution)/shard_map/ppermute | solution.py:463
  15.2 1.8 %collective-permute-start.8 = (bf16[128,128]{1,0:T(8,128)(2,1)S(1)}, bf16[128,128]{1,0:T(8,128)(2,1)S(1)}, u32[]{:S(2)}, u32[]{:S(2)}) collective-permute-start(bf16[128,128]{1,0:T(8,128)(2,1)S(1)} %get-tuple-element.87), channel_id=1, source_target_pairs={{0,1},{1,0},{2,3},{3,2},{4,5},{5,4},{6,7},{7,6},{8,9},{9,8},{10,11... | collective-permute-start | bytes 98312 | tf_op jit(solution)/shard_map/ppermute | solution.py:462
  17.0 0.0 collective-permute-done.4
  17.1 1.4 %collective-permute-start.5 = (bf16[120,128]{1,0:T(8,128)(2,1)S(1)}, bf16[120,128]{1,0:T(8,128)(2,1)S(1)}, u32[]{:S(2)}, u32[]{:S(2)}) collective-permute-start(bf16[120,128]{1,0:T(8,128)(2,1)S(1)} %get-tuple-element.118), channel_id=1, source_target_pairs={{0,12},{4,8},{8,4},{12,0},{16,28},{20,24},{24,20},{28,16},{1,13},{... | collective-permute-start | bytes 92168 | tf_op jit(solution)/shard_map/ppermute | solution.py:413
  18.5 1.0 %collective-permute-start.6 = (bf16[120,128]{1,0:T(8,128)(2,1)S(1)}, bf16[120,128]{1,0:T(8,128)(2,1)S(1)}, u32[]{:S(2)}, u32[]{:S(2)}) collective-permute-start(bf16[120,128]{1,0:T(8,128)(2,1)S(1)} %get-tuple-element.117), channel_id=1, source_target_pairs={{0,16},{4,20},{8,24},{12,28},{16,0},{20,4},{24,8},{28,12},{1,17},{... | collective-permute-start | bytes 92168 | tf_op jit(solution)/shard_map/ppermute | solution.py:413
  19.5 0.9 %collective-permute-start.7 = (bf16[120,128]{1,0:T(8,128)(2,1)S(1)}, bf16[120,128]{1,0:T(8,128)(2,1)S(1)}, u32[]{:S(2)}, u32[]{:S(2)}) collective-permute-start(bf16[120,128]{1,0:T(8,128)(2,1)S(1)} %get-tuple-element.116), channel_id=1, source_target_pairs={{0,28},{4,24},{8,20},{12,16},{16,12},{20,8},{24,4},{28,0},{1,29},{... | collective-permute-start | bytes 92168 | tf_op jit(solution)/shard_map/ppermute | solution.py:413
  20.3 0.4 collective-permute-start.12
  20.7 0.0 collective-permute-done.8.b2
  20.7 0.0 collective-permute-done.5
  20.7 0.5 %collective-permute-done.6 = bf16[120,128]{1,0:T(8,128)(2,1)S(1)} collective-permute-done((bf16[120,128]{1,0:T(8,128)(2,1)S(1)}, bf16[120,128]{1,0:T(8,128)(2,1)S(1)}, u32[]{:S(2)}, u32[]{:S(2)}) %collective-permute-start.6) | collective-permute-done | bytes 30752 | tf_op jit(solution)/shard_map/ppermute | solution.py:413
  21.2 2.5 %collective-permute-done.7 = bf16[120,128]{1,0:T(8,128)(2,1)S(1)} collective-permute-done((bf16[120,128]{1,0:T(8,128)(2,1)S(1)}, bf16[120,128]{1,0:T(8,128)(2,1)S(1)}, u32[]{:S(2)}, u32[]{:S(2)}) %collective-permute-start.7) | collective-permute-done | bytes 30752 | tf_op jit(solution)/shard_map/ppermute | solution.py:413
  23.7 1.5 %collective-permute-start.13 = (bf16[128,128]{1,0:T(8,128)(2,1)S(1)}, bf16[128,128]{1,0:T(8,128)(2,1)S(1)}, u32[]{:S(2)}, u32[]{:S(2)}) collective-permute-start(bf16[128,128]{1,0:T(8,128)(2,1)S(1)} %get-tuple-element.95), channel_id=1, source_target_pairs={{0,1},{1,0},{2,3},{3,2},{4,8},{5,9},{6,10},{7,11},{8,4},{9,5},{10,... | collective-permute-start | bytes 98312 | tf_op jit(solution)/shard_map/ppermute | solution.py:453
  25.2 2.0 %collective-permute-start.10 = (bf16[120,128]{1,0:T(8,128)(2,1)S(1)}, bf16[120,128]{1,0:T(8,128)(2,1)S(1)}, u32[]{:S(2)}, u32[]{:S(2)}) collective-permute-start(bf16[120,128]{1,0:T(8,128)(2,1)S(1)} %add_convert_fusion.1), channel_id=1, source_target_pairs={{0,6},{1,7},{2,4},{3,5},{4,2},{5,3},{6,0},{7,1},{8,14},{9,15},{10,... | collective-permute-start | bytes 92168 | tf_op jit(solution)/shard_map/ppermute | solution.py:395
  27.3 1.4 %collective-permute-start.11 = (bf16[120,128]{1,0:T(8,128)(2,1)S(1)}, bf16[120,128]{1,0:T(8,128)(2,1)S(1)}, u32[]{:S(2)}, u32[]{:S(2)}) collective-permute-start(bf16[120,128]{1,0:T(8,128)(2,1)S(1)} %add_convert_fusion.1), channel_id=1, source_target_pairs={{0,7},{1,6},{2,5},{3,4},{4,3},{5,2},{6,1},{7,0},{8,15},{9,14},{10,... | collective-permute-start | bytes 92168 | tf_op jit(solution)/shard_map/ppermute | solution.py:395
  28.6 0.0 collective-permute-start.9
  28.6 0.0 collective-permute-done.12.b3
  28.6 1.1 %collective-permute-done.10 = bf16[120,128]{1,0:T(8,128)(2,1)S(1)} collective-permute-done((bf16[120,128]{1,0:T(8,128)(2,1)S(1)}, bf16[120,128]{1,0:T(8,128)(2,1)S(1)}, u32[]{:S(2)}, u32[]{:S(2)}) %collective-permute-start.10) | collective-permute-done | bytes 30752 | tf_op jit(solution)/shard_map/ppermute | solution.py:395
  29.8 3.1 %collective-permute-done.11 = bf16[120,128]{1,0:T(8,128)(2,1)S(1)} collective-permute-done((bf16[120,128]{1,0:T(8,128)(2,1)S(1)}, bf16[120,128]{1,0:T(8,128)(2,1)S(1)}, u32[]{:S(2)}, u32[]{:S(2)}) %collective-permute-start.11) | collective-permute-done | bytes 30752 | tf_op jit(solution)/shard_map/ppermute | solution.py:395
  32.9 0.0 collective-permute-done.9
  32.9 0.0 collective-permute-done.13.b1
  32.9 0.8 %collective-permute-start.14 = (bf16[120,128]{1,0:T(8,128)(2,1)S(1)}, bf16[120,128]{1,0:T(8,128)(2,1)S(1)}, u32[]{:S(2)}, u32[]{:S(2)}) collective-permute-start(bf16[120,128]{1,0:T(8,128)(2,1)S(1)} %add_convert_fusion), channel_id=1, source_target_pairs={{0,12},{4,8},{8,4},{12,0},{16,28},{20,24},{24,20},{28,16},{1,13},{... | collective-permute-start | bytes 92168 | tf_op jit(solution)/shard_map/ppermute | solution.py:418
  33.7 0.5 %collective-permute-start.15 = (bf16[120,128]{1,0:T(8,128)(2,1)S(1)}, bf16[120,128]{1,0:T(8,128)(2,1)S(1)}, u32[]{:S(2)}, u32[]{:S(2)}) collective-permute-start(bf16[120,128]{1,0:T(8,128)(2,1)S(1)} %add_convert_fusion), channel_id=1, source_target_pairs={{0,16},{4,20},{8,24},{12,28},{16,0},{20,4},{24,8},{28,12},{1,17},{... | collective-permute-start | bytes 92168 | tf_op jit(solution)/shard_map/ppermute | solution.py:418
  34.2 2.0 %collective-permute-start.16 = (bf16[120,128]{1,0:T(8,128)(2,1)S(1)}, bf16[120,128]{1,0:T(8,128)(2,1)S(1)}, u32[]{:S(2)}, u32[]{:S(2)}) collective-permute-start(bf16[120,128]{1,0:T(8,128)(2,1)S(1)} %add_convert_fusion), channel_id=1, source_target_pairs={{0,28},{4,24},{8,20},{12,16},{16,12},{20,8},{24,4},{28,0},{1,29},{... | collective-permute-start | bytes 92168 | tf_op jit(solution)/shard_map/ppermute | solution.py:418
  36.2 0.7 %collective-permute-done.14 = bf16[120,128]{1,0:T(8,128)(2,1)S(1)} collective-permute-done((bf16[120,128]{1,0:T(8,128)(2,1)S(1)}, bf16[120,128]{1,0:T(8,128)(2,1)S(1)}, u32[]{:S(2)}, u32[]{:S(2)}) %collective-permute-start.14) | collective-permute-done | bytes 30752 | tf_op jit(solution)/shard_map/ppermute | solution.py:418
  36.9 0.0 collective-permute-done.15
  36.9 1.5 %collective-permute-done.16 = bf16[120,128]{1,0:T(8,128)(2,1)S(1)} collective-permute-done((bf16[120,128]{1,0:T(8,128)(2,1)S(1)}, bf16[120,128]{1,0:T(8,128)(2,1)S(1)}, u32[]{:S(2)}, u32[]{:S(2)}) %collective-permute-start.16) | collective-permute-done | bytes 30752 | tf_op jit(solution)/shard_map/ppermute | solution.py:418
  38.5 0.2 collective-permute-start.17
  38.7 0.9 %shard_map.258 = bf16[512,128]{1,0:T(8,128)(2,1)} custom-call(s32[4,128]{1,0:T(4,128)S(1)} %get-tuple-element.82.list_ref, bf16[128,128]{1,0:T(8,128)(2,1)S(1)} %slice.8.b0, bf16[128,128]{1,0:T(8,128)(2,1)S(1)} %collective-permute-done.13.b1, bf16[128,128]{1,0:T(8,128)(2,1)S(1)} %collective-permute-done.8.b2, bf16[128,128]{1,0:T(8,128)(2,1)S(1)} %collective-permute-done.12.b3), custom_call_target="tpu_custom_call" | custom-call | tf_op jit(solution)/shard_map/pallas_call | solution.py:580
  39.6 0.3 collective-permute-done.17.other
  39.9 1.0 %shard_map.259 = (f32[384,128]{1,0:T(8,128)}, f32[1,128]{1,0:T(1,128)}, f32[128,128]{1,0:T(8,128)}, f32[1,128]{1,0:T(1,128)}, f32[256,128]{1,0:T(8,128)}, /*inde...) custom-call(bf16[480,128]{1,0:T(8,128)(2,1)S(1)} %pad_maximum_fusion.2.mine, ...), custom_call_target="tpu_custom_call" | custom-call | tf_op jit(solution)/shard_map/pallas_call | solution.py:584
  (10 shorter events, 0.2 us)
Async XLA Ops:
  2.2 4.7 %collective-permute-start = (bf16[128,128]{1,0:T(8,128)(2,1)S(1)}, bf16[128,128]{1,0:T(8,128)(2,1)S(1)}, u32[]{:S(2)}, u32[]{:S(2)}) collective-permute-start(bf16[128,128]{1,0:T(8,128)(2,1)S(1)} %get-tuple-element.63), channel_id=1, source_target_pairs={{0,4},{4,0},{8,12},{12,8},{16,20},{20,16},{24,28},{28,24},{1,5},{5... | collective-permute-start | bytes 98312 | tf_op jit(solution)/shard_map/ppermute | solution.py:539
  2.3 4.6 %collective-permute-start.1 = (bf16[128,128]{1,0:T(8,128)(2,1)S(1)}, bf16[128,128]{1,0:T(8,128)(2,1)S(1)}, u32[]{:S(2)}, u32[]{:S(2)}) collective-permute-start(bf16[128,128]{1,0:T(8,128)(2,1)S(1)} %get-tuple-element.64), channel_id=1, source_target_pairs={{0,1},{1,0},{2,3},{3,2},{4,8},{5,9},{6,10},{7,11},{8,4},{9,5},{10,... | collective-permute-start | bytes 98312 | tf_op jit(solution)/shard_map/ppermute | solution.py:453
  4.9 2.8 %collective-permute-start.2 = (bf16[128,128]{1,0:T(8,128)(2,1)S(1)}, bf16[128,128]{1,0:T(8,128)(2,1)S(1)}, u32[]{:S(2)}, u32[]{:S(2)}) collective-permute-start(bf16[128,128]{1,0:T(8,128)(2,1)S(1)} %get-tuple-element.65), channel_id=1, source_target_pairs={{0,1},{1,0},{2,3},{3,2},{4,5},{5,4},{6,7},{7,6},{8,9},{9,8},{10,11... | collective-permute-start | bytes 98312 | tf_op jit(solution)/shard_map/ppermute | solution.py:541
  6.2 1.5 %collective-permute-start.3 = (bf16[128,128]{1,0:T(8,128)(2,1)S(1)}, bf16[128,128]{1,0:T(8,128)(2,1)S(1)}, u32[]{:S(2)}, u32[]{:S(2)}) collective-permute-start(bf16[128,128]{1,0:T(8,128)(2,1)S(1)} %get-tuple-element.66), channel_id=1, source_target_pairs={{0,4},{1,2},{2,1},{3,7},{4,0},{5,6},{6,5},{7,3},{8,12},{9,10},{10,... | collective-permute-start | bytes 98312 | tf_op jit(solution)/shard_map/ppermute | solution.py:453
  13.5 3.5 %collective-permute-start.4 = (bf16[608,128]{1,0:T(8,128)(2,1)S(1)}, bf16[608,128]{1,0:T(8,128)(2,1)S(1)}, u32[]{:S(2)}, u32[]{:S(2)}) collective-permute-start(bf16[608,128]{1,0:T(8,128)(2,1)S(1)} %pad_maximum_fusion), channel_id=1, source_target_pairs={{0,4},{4,0},{8,12},{12,8},{16,20},{20,16},{24,28},{28,24},{1,5},{5... | collective-permute-start | bytes 466952 | tf_op jit(solution)/shard_map/ppermute | solution.py:463
  15.2 5.6 %collective-permute-start.8 = (bf16[128,128]{1,0:T(8,128)(2,1)S(1)}, bf16[128,128]{1,0:T(8,128)(2,1)S(1)}, u32[]{:S(2)}, u32[]{:S(2)}) collective-permute-start(bf16[128,128]{1,0:T(8,128)(2,1)S(1)} %get-tuple-element.87), channel_id=1, source_target_pairs={{0,1},{1,0},{2,3},{3,2},{4,5},{5,4},{6,7},{7,6},{8,9},{9,8},{10,11... | collective-permute-start | bytes 98312 | tf_op jit(solution)/shard_map/ppermute | solution.py:462
  17.1 3.7 %collective-permute-start.5 = (bf16[120,128]{1,0:T(8,128)(2,1)S(1)}, bf16[120,128]{1,0:T(8,128)(2,1)S(1)}, u32[]{:S(2)}, u32[]{:S(2)}) collective-permute-start(bf16[120,128]{1,0:T(8,128)(2,1)S(1)} %get-tuple-element.118), channel_id=1, source_target_pairs={{0,12},{4,8},{8,4},{12,0},{16,28},{20,24},{24,20},{28,16},{1,13},{... | collective-permute-start | bytes 92168 | tf_op jit(solution)/shard_map/ppermute | solution.py:413
  18.5 2.7 %collective-permute-start.6 = (bf16[120,128]{1,0:T(8,128)(2,1)S(1)}, bf16[120,128]{1,0:T(8,128)(2,1)S(1)}, u32[]{:S(2)}, u32[]{:S(2)}) collective-permute-start(bf16[120,128]{1,0:T(8,128)(2,1)S(1)} %get-tuple-element.117), channel_id=1, source_target_pairs={{0,16},{4,20},{8,24},{12,28},{16,0},{20,4},{24,8},{28,12},{1,17},{... | collective-permute-start | bytes 92168 | tf_op jit(solution)/shard_map/ppermute | solution.py:413
  19.5 4.2 %collective-permute-start.7 = (bf16[120,128]{1,0:T(8,128)(2,1)S(1)}, bf16[120,128]{1,0:T(8,128)(2,1)S(1)}, u32[]{:S(2)}, u32[]{:S(2)}) collective-permute-start(bf16[120,128]{1,0:T(8,128)(2,1)S(1)} %get-tuple-element.116), channel_id=1, source_target_pairs={{0,28},{4,24},{8,20},{12,16},{16,12},{20,8},{24,4},{28,0},{1,29},{... | collective-permute-start | bytes 92168 | tf_op jit(solution)/shard_map/ppermute | solution.py:413
  20.3 8.3 %collective-permute-start.12 = (bf16[128,128]{1,0:T(8,128)(2,1)S(1)}, bf16[128,128]{1,0:T(8,128)(2,1)S(1)}, u32[]{:S(2)}, u32[]{:S(2)}) collective-permute-start(bf16[128,128]{1,0:T(8,128)(2,1)S(1)} %get-tuple-element.94), channel_id=1, source_target_pairs={{0,4},{1,2},{2,1},{3,7},{4,0},{5,6},{6,5},{7,3},{8,12},{9,10},{10,... | collective-permute-start | bytes 98312 | tf_op jit(solution)/shard_map/ppermute | solution.py:453
  23.7 9.1 %collective-permute-start.13 = (bf16[128,128]{1,0:T(8,128)(2,1)S(1)}, bf16[128,128]{1,0:T(8,128)(2,1)S(1)}, u32[]{:S(2)}, u32[]{:S(2)}) collective-permute-start(bf16[128,128]{1,0:T(8,128)(2,1)S(1)} %get-tuple-element.95), channel_id=1, source_target_pairs={{0,1},{1,0},{2,3},{3,2},{4,8},{5,9},{6,10},{7,11},{8,4},{9,5},{10,... | collective-permute-start | bytes 98312 | tf_op jit(solution)/shard_map/ppermute | solution.py:453
  25.2 4.5 %collective-permute-start.10 = (bf16[120,128]{1,0:T(8,128)(2,1)S(1)}, bf16[120,128]{1,0:T(8,128)(2,1)S(1)}, u32[]{:S(2)}, u32[]{:S(2)}) collective-permute-start(bf16[120,128]{1,0:T(8,128)(2,1)S(1)} %add_convert_fusion.1), channel_id=1, source_target_pairs={{0,6},{1,7},{2,4},{3,5},{4,2},{5,3},{6,0},{7,1},{8,14},{9,15},{10,... | collective-permute-start | bytes 92168 | tf_op jit(solution)/shard_map/ppermute | solution.py:395
  27.3 5.6 %collective-permute-start.11 = (bf16[120,128]{1,0:T(8,128)(2,1)S(1)}, bf16[120,128]{1,0:T(8,128)(2,1)S(1)}, u32[]{:S(2)}, u32[]{:S(2)}) collective-permute-start(bf16[120,128]{1,0:T(8,128)(2,1)S(1)} %add_convert_fusion.1), channel_id=1, source_target_pairs={{0,7},{1,6},{2,5},{3,4},{4,3},{5,2},{6,1},{7,0},{8,15},{9,14},{10,... | collective-permute-start | bytes 92168 | tf_op jit(solution)/shard_map/ppermute | solution.py:395
  28.6 4.2 %collective-permute-start.9 = (bf16[120,128]{1,0:T(8,128)(2,1)S(1)}, bf16[120,128]{1,0:T(8,128)(2,1)S(1)}, u32[]{:S(2)}, u32[]{:S(2)}) collective-permute-start(bf16[120,128]{1,0:T(8,128)(2,1)S(1)} %add_convert_fusion.1), channel_id=1, source_target_pairs={{0,1},{1,0},{2,3},{3,2},{4,5},{5,4},{6,7},{7,6},{8,9},{9,8},{10,11... | collective-permute-start | bytes 92168 | tf_op jit(solution)/shard_map/ppermute | solution.py:395
  32.9 4.0 %collective-permute-start.14 = (bf16[120,128]{1,0:T(8,128)(2,1)S(1)}, bf16[120,128]{1,0:T(8,128)(2,1)S(1)}, u32[]{:S(2)}, u32[]{:S(2)}) collective-permute-start(bf16[120,128]{1,0:T(8,128)(2,1)S(1)} %add_convert_fusion), channel_id=1, source_target_pairs={{0,12},{4,8},{8,4},{12,0},{16,28},{20,24},{24,20},{28,16},{1,13},{... | collective-permute-start | bytes 92168 | tf_op jit(solution)/shard_map/ppermute | solution.py:418
  33.7 3.2 %collective-permute-start.15 = (bf16[120,128]{1,0:T(8,128)(2,1)S(1)}, bf16[120,128]{1,0:T(8,128)(2,1)S(1)}, u32[]{:S(2)}, u32[]{:S(2)}) collective-permute-start(bf16[120,128]{1,0:T(8,128)(2,1)S(1)} %add_convert_fusion), channel_id=1, source_target_pairs={{0,16},{4,20},{8,24},{12,28},{16,0},{20,4},{24,8},{28,12},{1,17},{... | collective-permute-start | bytes 92168 | tf_op jit(solution)/shard_map/ppermute | solution.py:418
  34.2 4.2 %collective-permute-start.16 = (bf16[120,128]{1,0:T(8,128)(2,1)S(1)}, bf16[120,128]{1,0:T(8,128)(2,1)S(1)}, u32[]{:S(2)}, u32[]{:S(2)}) collective-permute-start(bf16[120,128]{1,0:T(8,128)(2,1)S(1)} %add_convert_fusion), channel_id=1, source_target_pairs={{0,28},{4,24},{8,20},{12,16},{16,12},{20,8},{24,4},{28,0},{1,29},{... | collective-permute-start | bytes 92168 | tf_op jit(solution)/shard_map/ppermute | solution.py:418
  38.5 1.4 %collective-permute-start.17 = (bf16[480,128]{1,0:T(8,128)(2,1)S(1)}, bf16[480,128]{1,0:T(8,128)(2,1)S(1)}, u32[]{:S(2)}, u32[]{:S(2)}) collective-permute-start(bf16[480,128]{1,0:T(8,128)(2,1)S(1)} %pad_maximum_fusion.2.mine), channel_id=1, source_target_pairs={{0,4},{4,0},{8,12},{12,8},{16,20},{20,16},{24,28},{28,24},{1,5},{5... | collective-permute-start | bytes 368648 | tf_op jit(solution)/shard_map/ppermute | solution.py:581
